TPU v7x, 256 devices: a whole 4x4x8 slice. The times are simulated.
256 devices in a mesh: tm: 8 (over z), par: 32 (over x, y, core).
Axes of the slice: x: 4, y: 4, z: 8, core: 2. Of those that a mesh axis runs over, the one named last changes fastest.
Arguments:
- kernel: bfloat16 [128, 256, 4096], P('tm', None, 'par'), may hold values from -0.015625 to 0.015625
- history: bfloat16 [128, 4096, 128], P('tm', 'par'), may hold values from -6 to 6
- arrivals: bfloat16 [2, 16, 4096, 128], P(None, 'tm', 'par'), may hold values from -6 to 6
Outputs:
- observations: bfloat16 [2, 16, 256, 128], P(None, None, ('tm', 'par'))
All inputs are finite; a program needn't handle non-finite values.
Results may differ from a plain program's by a relative error of at most 0.014.
Values may be sent and summed in bfloat16 or wider, within the bound.
A program may use at most 64 MiB of HBM per device.

v0:
```python
import math

import jax
import jax.numpy as jnp
from jax import lax
from jax.sharding import Mesh
from jax.sharding import PartitionSpec as P

TM_PAR = ("tm", "par_0", "par_1", "par_2")
PAR = ("par_0", "par_1", "par_2")


def from_everyone(array, axis):
    copies = jnp.broadcast_to(array, (lax.axis_size(axis), *array.shape))
    return lax.all_to_all(copies, axis, split_axis=0, concat_axis=0, tiled=True)


def laid_out(parts, dim):
    lengths = list(parts.shape[1:])
    lengths[dim] *= parts.shape[0]
    return jnp.moveaxis(parts, 0, dim).reshape(lengths)


def gathered_copies(array, axis, dim):
    parts = from_everyone(array, axis)
    return laid_out(parts, dim)


def from_behind(array, axis, by):
    size = lax.axis_size(axis)
    pairs = [(i, i + by) for i in range(size) if 0 <= i + by < size]
    return lax.ppermute(array, axis, pairs)


def split_up(array, dim, size):
    lengths = array.shape
    parts = array.reshape(*lengths[:dim], size, lengths[dim] // size, *lengths[dim + 1 :])
    return jnp.moveaxis(parts, dim, 0)


def sent_and_summed(array, axis, dim):
    parts = split_up(array, dim, lax.axis_size(axis))
    arrived = lax.all_to_all(parts, axis, split_axis=0, concat_axis=0, tiled=True)
    return arrived.astype(jnp.float32).sum(axis=0)


def sum_by_axis(array, axes, dim):
    far, near = axes
    parts = split_up(array, dim, lax.axis_size(far))
    nearer = sent_and_summed(parts, near, dim + 1)
    arrived = lax.all_to_all(
        nearer.astype(jnp.bfloat16), far, split_axis=0, concat_axis=0, tiled=True
    )
    return arrived.astype(jnp.float32).sum(axis=0)


def tables(block_len):
    length = 2 * block_len
    freq_count = block_len + 1
    freq_index = lax.broadcasted_iota(jnp.int32, (freq_count, length), 0)
    time_index = lax.broadcasted_iota(jnp.int32, (freq_count, length), 1)
    angles = (freq_index * time_index % length).astype(jnp.float32) * (2.0 * math.pi / length)
    forward = jnp.concatenate([jnp.cos(angles), -jnp.sin(angles)], 0)
    forward_high = forward.astype(jnp.bfloat16)
    forward_low = (forward - forward_high.astype(jnp.float32)).astype(jnp.bfloat16)
    out_index = lax.broadcasted_iota(jnp.int32, (block_len, freq_count), 0) + block_len
    spec_index = lax.broadcasted_iota(jnp.int32, (block_len, freq_count), 1)
    out_angles = (out_index * spec_index % length).astype(jnp.float32) * (2.0 * math.pi / length)
    edge_freq = (spec_index == 0) | (spec_index == block_len)
    cos_weight = jnp.where(edge_freq, 1.0, 2.0) / length
    sin_weight = jnp.where(edge_freq, 0.0, 2.0) / length
    inverse = jnp.concatenate(
        [cos_weight * jnp.cos(out_angles), -sin_weight * jnp.sin(out_angles)], 1
    )
    return ((forward_high, forward_low), inverse)


def transform(table_pair, data):
    high_part = jnp.dot(table_pair[0], data, preferred_element_type=jnp.float32)
    return high_part + jnp.dot(table_pair[1], data, preferred_element_type=jnp.float32)


def product(left_operand, right_operand):
    return jnp.einsum(
        "njy,nyv->njv", left_operand, right_operand, preferred_element_type=jnp.float32
    )


def observe(older_block, newer_block, spectrum, forward, inverse):
    block_len, params, fields = older_block.shape
    freq_count = block_len + 1
    sensors = spectrum.shape[2]
    window = jnp.concatenate([older_block, newer_block], 0)
    window = window.reshape(2 * block_len, params * fields)
    window_spec = transform(forward, window)
    window_spec = window_spec.astype(jnp.bfloat16).reshape(2, freq_count, params, fields)
    real_component = product(spectrum[0], window_spec[0]) - product(spectrum[1], window_spec[1])
    imaginary_component = product(spectrum[0], window_spec[1]) + product(
        spectrum[1], window_spec[0]
    )
    stacked = jnp.concatenate([real_component, imaginary_component], 0).reshape(
        2 * freq_count, sensors * fields
    )
    signal = jnp.dot(inverse, stacked, preferred_element_type=jnp.float32)
    return signal.reshape(block_len, sensors, fields)


def per_device(kernel, history, arrivals):
    block_len, sensors, params = kernel.shape
    step_count = arrivals.shape[0]
    freq_count = block_len + 1
    forward, inverse = tables(block_len)
    kernel_flat = kernel.reshape(block_len, sensors * params)
    lag_tables = (forward[0][:, :block_len], forward[1][:, :block_len])
    spectrum = transform(lag_tables, kernel_flat)
    spectrum = spectrum.astype(jnp.bfloat16).reshape(2, freq_count, sensors, params)
    incoming = gathered_copies(arrivals, "tm", 1)
    position = lax.axis_index("tm")
    partials = []
    older_block = history
    for step_index in range(step_count):
        shifted = from_behind(older_block, "tm", 1)
        newer_block = jnp.where(position == 0, incoming[step_index], shifted)
        partials.append(observe(older_block, newer_block, spectrum, forward, inverse))
        older_block = newer_block
    result = sum_by_axis(
        jnp.stack(partials, 0).astype(jnp.bfloat16), (("tm", "par_0"), ("par_1", "par_2")), 2
    ).astype(jnp.bfloat16)
    return result


def solution(mesh):
    split = Mesh(mesh.devices.reshape(mesh.shape["tm"], 4, 4, 2), ("tm", "par_0", "par_1", "par_2"))
    placed = (P("tm", None, PAR), P("tm", PAR, None), P(None, "tm", PAR, None))
    return jax.shard_map(
        per_device,
        mesh=split,
        in_specs=placed,
        out_specs=P(None, None, TM_PAR, None),
        check_vma=False,
    )
```

profile of v0, /device:TPU:1, one launch (start us, length us, event | category | flops | bytes accessed | tf_op | source)
XLA Modules:
  0.0 128.7 jit_solution(15863421673612094853)
XLA Ops:
  0.0 2.3 %broadcast_in_dim.18 = bf16[8,2,2,128,128]{4,3,2,1,0:T(8,128)(2,1)} broadcast(bf16[2,2,128,128]{3,2,1,0:T(8,128)(2,1)} %param.5), dimensions={1,2,3,4} | broadcast | bytes 1179648 | tf_op jit(solution)/shard_map/broadcast_in_dim | solution.py:14
  2.3 9.0 %all-to-all-start = ((bf16[8,2,2,128,128]{4,3,2,1,0:T(8,128)(2,1)}), bf16[8,2,2,128,128]{4,3,2,1,0:T(8,128)(2,1)}, u32[]{:S(2)}, u32[]{:S(2)}) async-start(bf16[8,2,2,128,128]{4,3,2,1,0:T(8,128)(2,1)} %broadcast_in_dim.18), calls=%async_computation | async-start | bytes 2097152 | tf_op jit(solution)/shard_map/all_to_all | solution.py:15
  11.3 4.2 %collective-permute-start = (bf16[16,128,128]{2,1,0:T(8,128)(2,1)S(1)}, bf16[16,128,128]{2,1,0:T(8,128)(2,1)}, u32[]{:S(2)}, u32[]{:S(2)}) collective-permute-start(bf16[16,128,128]{2,1,0:T(8,128)(2,1)S(1)} %copy-done.2), channel_id=1, source_target_pairs={{0,32},{32,64},{64,96},{96,128},{128,160},{160,192},{192,224},{1,3... | collective-permute-start | bytes 1572872 | tf_op jit(solution)/shard_map/ppermute | solution.py:32
  15.6 0.9 fusion.26
  16.8 0.9 fusion
  17.8 22.8 %all-to-all-done = bf16[8,2,2,128,128]{4,3,2,1,0:T(8,128)(2,1)} async-done(((bf16[8,2,2,128,128]{4,3,2,1,0:T(8,128)(2,1)}), bf16[8,2,2,128,128]{4,3,2,1,0:T(8,128)(2,1)}, u32[]{:S(2)}, u32[]{:S(2)}) %all-to-all-start) | async-done | bytes 1048608 | tf_op jit(solution)/shard_map/all_to_all | solution.py:15
  40.6 1.3 fusion.76
  41.9 2.7 %collective-permute-done = bf16[16,128,128]{2,1,0:T(8,128)(2,1)} collective-permute-done((bf16[16,128,128]{2,1,0:T(8,128)(2,1)S(1)}, bf16[16,128,128]{2,1,0:T(8,128)(2,1)}, u32[]{:S(2)}, u32[]{:S(2)}) %collective-permute-start) | collective-permute-done | bytes 524320 | tf_op jit(solution)/shard_map/ppermute | solution.py:32
  44.7 5.4 %collective-permute-start.1 = (bf16[16,128,128]{2,1,0:T(8,128)(2,1)S(1)}, bf16[16,128,128]{2,1,0:T(8,128)(2,1)S(1)}, u32[]{:S(2)}, u32[]{:S(2)}) collective-permute-start(bf16[16,128,128]{2,1,0:T(8,128)(2,1)S(1)} %bitcast_select_fusion.1), channel_id=1, source_target_pairs={{0,32},{32,64},{64,96},{96,128},{128,160},{160,192},{192,224},{1,3... | collective-permute-start | bytes 1572872 | tf_op jit(solution)/shard_map/ppermute | solution.py:32
  51.4 8.3 %collective-permute-done.1 = bf16[16,128,128]{2,1,0:T(8,128)(2,1)S(1)} collective-permute-done((bf16[16,128,128]{2,1,0:T(8,128)(2,1)S(1)}, bf16[16,128,128]{2,1,0:T(8,128)(2,1)S(1)}, u32[]{:S(2)}, u32[]{:S(2)}) %collective-permute-start.1) | collective-permute-done | bytes 524320 | tf_op jit(solution)/shard_map/ppermute | solution.py:32
  60.0 0.8 fusion.20
  60.8 0.8 fusion.2
  63.1 0.5 convolution_add_fusion.3
  63.5 0.5 convolution_subtract_fusion
  64.4 0.8 fusion.23
  65.2 0.8 fusion.1
  67.5 0.5 convolution_add_fusion.4
  67.9 0.5 convolution_subtract_fusion.1
  68.9 1.6 %fusion.13 = bf16[1,16,32,8,128]{4,1,3,2,0:T(8,128)(2,1)S(1)} fusion(bf16[32,8,128,34]{2,1,0,3:T(8,128)(2,1)S(1)} %slice_bitcast_fusion, bf16[16,17]{1,0:T(8,128)(2,1)S(1)} %get-tuple-element.18, bf16[16,17]{1,0:T(8,128)(2,1)S(1)} %get-tuple-element.17), kind=kOutput, calls=%fused_computation.21 | convolution fusion | flops 35653760 | bytes 3277888 | tf_op jit(solution)/shard_map/dot_general | solution.py:104
  70.5 1.6 %fusion.16 = bf16[1,16,32,8,128]{4,1,3,2,0:T(8,128)(2,1)S(1)} fusion(bf16[32,8,128,34]{2,1,0,3:T(8,128)(2,1)S(1)} %slice_bitcast_fusion.1, bf16[16,17]{1,0:T(8,128)(2,1)S(1)} %get-tuple-element.18, bf16[16,17]{1,0:T(8,128)(2,1)S(1)} %get-tuple-element.17), kind=kOutput, calls=%fused_computation.22 | convolution fusion | flops 35653760 | bytes 3277888 | tf_op jit(solution)/shard_map/dot_general | solution.py:104
  72.3 0.5 copy.8
  72.8 32.8 %all_to_all.15 = bf16[8,32,2,16,1,128]{5,3,1,2,4,0:T(8,128)(2,1)S(1)} all-to-all(bf16[8,32,2,16,1,128]{5,3,1,2,4,0:T(8,128)(2,1)S(1)} %copy.8), channel_id=1, replica_groups=mesh['tm'=8,'par_0'=4,'par_1'=4,'par_2'=2] {'par_1','par_2'}, dimensions={0} | all-to-all | bytes 4194304 | tf_op jit(solution)/shard_map/all_to_all | solution.py:43
  106.0 22.0 %all_to_all.16 = bf16[32,2,16,1,128]{4,2,1,3,0:T(8,128)(2,1)S(1)} all-to-all(bf16[32,2,16,1,128]{4,2,1,3,0:T(8,128)(2,1)S(1)} %copy.10), channel_id=1, replica_groups=mesh['tm'=8,'par_0'=4,'par_1'=4,'par_2'=2] {'tm','par_0'}, dimensions={0} | all-to-all | bytes 524288 | tf_op jit(solution)/shard_map/all_to_all | solution.py:51
  128.1 0.6 reduce_sum.30
  (34 shorter events, 6.3 us)
Async XLA Ops:
  0.0 11.3 %copy-start.2 = (bf16[16,128,128]{2,1,0:T(8,128)(2,1)S(1)}, bf16[16,128,128]{2,1,0:T(8,128)(2,1)}, u32[]{:S(2)}) copy-start(bf16[16,128,128]{2,1,0:T(8,128)(2,1)} %param.4) | copy-start | bytes 1572868
  0.0 15.6 %copy-start = (bf16[16,256,128]{2,1,0:T(8,128)(2,1)S(1)}, bf16[16,256,128]{2,1,0:T(8,128)(2,1)}, u32[]{:S(2)}) copy-start(bf16[16,256,128]{2,1,0:T(8,128)(2,1)} %param.3) | copy-start | bytes 3145732
  2.3 38.3 %all-to-all-start = ((bf16[8,2,2,128,128]{4,3,2,1,0:T(8,128)(2,1)}), bf16[8,2,2,128,128]{4,3,2,1,0:T(8,128)(2,1)}, u32[]{:S(2)}, u32[]{:S(2)}) async-start(bf16[8,2,2,128,128]{4,3,2,1,0:T(8,128)(2,1)} %broadcast_in_dim.18), calls=%async_computation | async-start | bytes 2097152 | tf_op jit(solution)/shard_map/all_to_all | solution.py:15
  11.3 33.3 %collective-permute-start = (bf16[16,128,128]{2,1,0:T(8,128)(2,1)S(1)}, bf16[16,128,128]{2,1,0:T(8,128)(2,1)}, u32[]{:S(2)}, u32[]{:S(2)}) collective-permute-start(bf16[16,128,128]{2,1,0:T(8,128)(2,1)S(1)} %copy-done.2), channel_id=1, source_target_pairs={{0,32},{32,64},{64,96},{96,128},{128,160},{160,192},{192,224},{1,3... | collective-permute-start | bytes 1572872 | tf_op jit(solution)/shard_map/ppermute | solution.py:32
  15.6 1.2 copy-start.1
  44.7 15.0 %collective-permute-start.1 = (bf16[16,128,128]{2,1,0:T(8,128)(2,1)S(1)}, bf16[16,128,128]{2,1,0:T(8,128)(2,1)S(1)}, u32[]{:S(2)}, u32[]{:S(2)}) collective-permute-start(bf16[16,128,128]{2,1,0:T(8,128)(2,1)S(1)} %bitcast_select_fusion.1), channel_id=1, source_target_pairs={{0,32},{32,64},{64,96},{96,128},{128,160},{160,192},{192,224},{1,3... | collective-permute-start | bytes 1572872 | tf_op jit(solution)/shard_map/ppermute | solution.py:32
where the time goes:
time: 130 us; the launch traced here: 129 us
  blocking collectives  54.9 us (42%)
  waiting for transfers between devices  33.9 us (26%)
  starting transfers between devices  18.6 us (14%)
  matrix products  11.8 us (9%)
  local copies, waits for them, and re-layouts  7.02 us (5%)
  other arithmetic  2.27 us (2%)
    all_to_all x1, blocking collectives, sent_and_summed(): lax.all_to_all(parts, axis, split_axis=0, concat_axis=0, tiled=True)  32.8 us
    all_to_all x1, waiting for transfers between devices, from_everyone(): return lax.all_to_all(copies, axis, split_axis=0, concat_axis=0, tiled=True)  22.8 us
    all_to_all x1, blocking collectives, sum_by_axis(): lax.all_to_all(nearer.astype(jnp.bfloat16), far, split_axis=0, concat_axi...  22 us
    ppermute x2, waiting for transfers between devices, from_behind(): return lax.ppermute(array, axis, pairs)  11 us
    ppermute x2, starting transfers between devices, from_behind(): return lax.ppermute(array, axis, pairs)  9.59 us
    all_to_all x1, starting transfers between devices, from_everyone(): return lax.all_to_all(copies, axis, split_axis=0, concat_axis=0, tiled=True)  9 us
    dot_general x8, matrix products, product(): jnp.einsum('njy,nyv->njv', left_operand, right_operand, preferred_element...  3.6 us
    dot_general x2, matrix products, observe(): signal = jnp.dot(inverse, stacked, preferred_element_type=jnp.float32)  3.2 us
  transfers between devices with their start and end apart: 3, of which 3 were waited for; matrix products, arithmetic and copies ran while one was open for 3% of the time, Pallas kernels for 0%

commit v1 on v0

v1 whole, which is shorter than its diff:
```python
import jax
import jax.numpy as jnp
from jax import lax
from jax.experimental import pallas as pl
from jax.experimental.pallas import tpu as pltpu
from jax.sharding import Mesh
from jax.sharding import PartitionSpec as P

PAR = ("px", "py", "pc")
MESH = pl.DeviceIdType.MESH
CHUNK = 4
PIECE = 2


def kernel(k_hbm, h_hbm, a_hbm, out_ref, kv, krev, w, w2, relay, d2s, d2o, d2r, s1, o1, r1, s2, o2, r2, yb, zs, zo, zr,
           local_sem, w_recv, own_send, fwd_send, arr_send, relay_recv, relay_send, d2_send, d2_recv,
           s1_send, s1_recv, s2_send, s2_recv, z_send, z_recv):
    z, x, y, c = (lax.axis_index(name) for name in ("tm", "px", "py", "pc"))
    nz, nx, ny, nc = 8, 4, 4, 2
    steps = 32
    chunks = steps // CHUNK
    lanes = CHUNK * 128
    sizes = {"tm": nz, "px": nx, "py": ny, "pc": nc}
    here = {"tm": z, "px": x, "py": y, "pc": c}

    def ahead(name, by):
        return {name: lax.rem(here[name] + by, sizes[name])}

    copy_k = pltpu.make_async_copy(k_hbm, kv, local_sem.at[0])
    copy_k.start()
    copy_h = pltpu.make_async_copy(h_hbm, w.at[pl.ds(0, 16)], local_sem.at[1])
    copy_h.start()

    barrier = pltpu.get_barrier_semaphore()
    peers = [(name, by) for name in sizes for by in range(1, sizes[name])]
    for name, by in peers:
        pl.semaphore_signal(barrier, inc=1, device_id=ahead(name, by), device_id_type=MESH)
    pl.semaphore_wait(barrier, len(peers))

    def remote(src, dst, send_sem, recv_sem, target):
        return pltpu.make_async_remote_copy(
            src_ref=src, dst_ref=dst, send_sem=send_sem, recv_sem=recv_sem, device_id=target, device_id_type=MESH
        )

    def own_piece(i):
        return remote(h_hbm.at[pl.ds(2 * i, 2)], w.at[pl.ds(16 + 2 * i, 2)], own_send.at[i], w_recv.at[0, i], ahead("tm", 1))

    def forward_piece(i):
        return remote(
            w.at[pl.ds(16 + 2 * i, 2)], w.at[pl.ds(32 + 2 * i, 2)], fwd_send.at[i], w_recv.at[1, i], ahead("tm", 1)
        )

    def wait_piece(blk, i):
        ref = w.at[pl.ds(16 + 16 * blk + 2 * i, 2)]
        remote(ref, ref, fwd_send.at[i], w_recv.at[blk, i], ahead("tm", 1)).wait_recv()

    def arrival_piece(s, owner):
        return remote(
            a_hbm.at[s], w.at[pl.ds(16 + 16 * s + 2 * owner, 2)], arr_send.at[s], w_recv.at[s, owner], {"tm": 0}
        )

    def to_relay(s):
        return remote(a_hbm.at[s], relay.at[s], arr_send.at[s], relay_recv.at[s], ahead("tm", nz - 3))

    def from_relay(s, owner):
        return remote(
            relay.at[s], w.at[pl.ds(16 + 16 * s + 2 * owner, 2)], relay_send.at[s], w_recv.at[s, owner], {"tm": 0}
        )

    def local_arrival(s):
        return pltpu.make_async_copy(a_hbm.at[s], w.at[pl.ds(16 + 16 * s, 2)], w_recv.at[s, 0])

    @pl.when(z == 0)
    def _():
        for s in range(2):
            local_arrival(s).start()

    @pl.when(z < nz - 1)
    def _():
        for i in range(8):
            own_piece(i).start()

    for s in range(2):
        for owner in (1, 2, 3, 7):

            @pl.when(z == owner)
            def _():
                arrival_piece(s, owner).start()

        @pl.when((z >= 4) & (z <= 6))
        def _():
            to_relay(s).start()

    row = lax.broadcasted_iota(jnp.int32, (256, 256), 0)
    col = lax.broadcasted_iota(jnp.int32, (256, 256), 1)
    core_of = (c + (row >> 7)) & 1
    x_of = (x + (row >> 5)) & 3
    y_of = (y + (row >> 3)) & 3
    z_of = (z + row) & 7
    sensor = z_of * 32 + x_of * 8 + y_of * 2 + core_of
    order = jnp.where(sensor == col, 1.0, 0.0).astype(jnp.bfloat16)
    copy_k.wait()
    for lag in range(16):
        moved = jnp.dot(order, kv[lag], preferred_element_type=jnp.float32)
        krev[:, (15 - lag) * 128 : (16 - lag) * 128] = moved.astype(jnp.bfloat16)

    def place(t):
        block = w[t]
        w2[t * 128 : (t + 1) * 128, 0:128] = block
        if t > 0:
            w2[(t - 1) * 128 : t * 128, 128:256] = block

    copy_h.wait()
    for t in range(16):
        place(t)

    def order_of(g):
        return ("px", "py") if g % 2 == 0 else ("py", "px")

    def core_copy(g):
        return remote(d2s.at[g], d2r.at[g], d2_send.at[g], d2_recv.at[g], ahead("pc", 1))

    def first_copy(g, d):
        return remote(
            s1.at[g, d - 1], r1.at[g, d - 1], s1_send.at[g, d - 1], s1_recv.at[g, d - 1], ahead(order_of(g)[0], d)
        )

    def second_copy(g, d):
        return remote(
            s2.at[g, d - 1], r2.at[g, d - 1], s2_send.at[g, d - 1], s2_recv.at[g, d - 1], ahead(order_of(g)[1], d)
        )

    def z_copy(s, d):
        return remote(zs.at[s, d - 1], zr.at[s, d - 1], z_send.at[s, d - 1], z_recv.at[s, d - 1], ahead("tm", d))

    def compute(g):
        blk = g // 4
        for i in (2 * (g % 4), 2 * (g % 4) + 1):
            wait_piece(blk, i)
            if blk == 0:

                @pl.when(z < nz - 1)
                def _():
                    forward_piece(i).start()

            for t in range(16 + 16 * blk + 2 * i, 18 + 16 * blk + 2 * i):
                place(t)
        for pair in range(CHUNK // 2):
            m = CHUNK * g + 2 * pair
            found = jnp.dot(krev[...], w2[(m + 1) * 128 : (m + 17) * 128, :], preferred_element_type=jnp.float32)
            d2s[g, :, pair * 256 : (pair + 1) * 256] = found[128:].astype(jnp.bfloat16)
            d2o[g, :, pair * 256 : (pair + 1) * 256] = found[:128]
        core_copy(g).start()

    def fold(block):
        half = lanes // 2
        return jnp.concatenate([block[:, :half], block[:, half:]], axis=0)

    def after_core(g):
        core_copy(g).wait_recv()
        total = d2o[g] + d2r[g].astype(jnp.float32)
        for d in range(4):
            if order_of(g)[0] == "px":
                block = total[32 * d : 32 * d + 32]
            else:
                block = jnp.concatenate([total[32 * e + 8 * d : 32 * e + 8 * d + 8] for e in range(4)], axis=0)
            if d == 0:
                o1[g] = block
            else:
                s1[g, d - 1] = block.astype(jnp.bfloat16)
        for d in (2, 1, 3):
            first_copy(g, d).start()

    def after_first(g):
        total = o1[g]
        for d in (1, 3, 2):
            first_copy(g, d).wait_recv()
            total = total + r1[g, d - 1].astype(jnp.float32)
        for d in range(4):
            block = fold(total[8 * d : 8 * d + 8])
            if d == 0:
                o2[g] = block
            else:
                s2[g, d - 1] = block.astype(jnp.bfloat16)
        for d in (2, 1, 3):
            second_copy(g, d).start()

    def after_second(g):
        total = o2[g]
        for d in (1, 3, 2):
            second_copy(g, d).wait_recv()
            total = total + r2[g, d - 1].astype(jnp.float32)
        for high in range(2):
            for low in range(CHUNK // 2):
                m = CHUNK * g + high * (CHUNK // 2) + low
                yb[m * 8 : m * 8 + 8, :] = total[high * 8 : high * 8 + 8, low * 128 : (low + 1) * 128]

    def send_z(s):
        for d in range(8):
            rows = yb[pl.ds(s * 128 + d, 16, stride=8), :]
            if d == 0:
                zo[s] = rows
            else:
                zs[s, d - 1] = rows.astype(jnp.bfloat16)
        for d in (4, 3, 5, 2, 6, 1, 7):
            z_copy(s, d).start()

    def finish(s):
        total = zo[s]
        for d in range(1, 8):
            z_copy(s, d).wait_recv()
            total = total + zr[s, d - 1].astype(jnp.float32)
        out_ref[s * 16 : (s + 1) * 16, :] = total.astype(jnp.bfloat16)

    def relay_on(s):
        for owner in (4, 5, 6):

            @pl.when(z == owner - 3)
            def _():
                to_relay(s).wait_recv()
                from_relay(s, owner).start()

    for step in range(chunks + 5):
        if step < chunks:
            compute(step)
        if step == 1:
            relay_on(0)
        if step == 2:
            relay_on(1)
        if 0 <= step - 1 < chunks:
            after_core(step - 1)
        if 0 <= step - 3 < chunks:
            after_first(step - 3)
        if 0 <= step - 5 < chunks:
            after_second(step - 5)
        if step - 5 == chunks // 2 - 1:
            send_z(0)
    send_z(1)
    finish(0)
    finish(1)

    @pl.when(z < nz - 1)
    def _():
        for i in range(8):
            own_piece(i).wait_send()
            forward_piece(i).wait_send()

    for s in range(2):
        for owner in (1, 2, 3, 7):

            @pl.when(z == owner)
            def _():
                arrival_piece(s, owner).wait_send()

        for owner in (4, 5, 6):

            @pl.when(z == owner)
            def _():
                to_relay(s).wait_send()

            @pl.when(z == owner - 3)
            def _():
                from_relay(s, owner).wait_send()

    for g in range(chunks):
        core_copy(g).wait_send()
        for d in range(1, 4):
            first_copy(g, d).wait_send()
            second_copy(g, d).wait_send()
    for s in range(2):
        for d in range(1, 8):
            z_copy(s, d).wait_send()


def per_device(lags, history, arrivals):
    chunks = 32 // CHUNK
    lanes = CHUNK * 128
    bf16, f32 = jnp.bfloat16, jnp.float32
    dma = pltpu.SemaphoreType.DMA
    found = pl.pallas_call(
        kernel,
        out_shape=jax.ShapeDtypeStruct((32, 128), bf16),
        in_specs=[pl.BlockSpec(memory_space=pl.ANY)] * 3,
        out_specs=pl.BlockSpec(memory_space=pltpu.VMEM),
        scratch_shapes=[
            pltpu.VMEM((16, 256, 128), bf16),
            pltpu.VMEM((256, 2048), bf16),
            pltpu.VMEM((48, 128, 128), bf16),
            pltpu.VMEM((48 * 128, 256), bf16),
            pltpu.VMEM((2, 2, 128, 128), bf16),
            pltpu.VMEM((chunks, 128, lanes), bf16),
            pltpu.VMEM((chunks, 128, lanes), f32),
            pltpu.VMEM((chunks, 128, lanes), bf16),
            pltpu.VMEM((chunks, 3, 32, lanes), bf16),
            pltpu.VMEM((chunks, 32, lanes), f32),
            pltpu.VMEM((chunks, 3, 32, lanes), bf16),
            pltpu.VMEM((chunks, 3, 16, lanes // 2), bf16),
            pltpu.VMEM((chunks, 16, lanes // 2), f32),
            pltpu.VMEM((chunks, 3, 16, lanes // 2), bf16),
            pltpu.VMEM((256, 128), f32),
            pltpu.VMEM((2, 7, 16, 128), bf16),
            pltpu.VMEM((2, 16, 128), f32),
            pltpu.VMEM((2, 7, 16, 128), bf16),
            dma((2,)),
            dma((2, 8)),
            dma((8,)),
            dma((8,)),
            dma((2,)),
            dma((2,)),
            dma((2,)),
            dma((chunks,)),
            dma((chunks,)),
            dma((chunks, 3)),
            dma((chunks, 3)),
            dma((chunks, 3)),
            dma((chunks, 3)),
            dma((2, 7)),
            dma((2, 7)),
        ],
        compiler_params=pltpu.CompilerParams(
            collective_id=0, has_side_effects=True, vmem_limit_bytes=48 * 1024 * 1024
        ),
    )(lags, history, arrivals)
    return found.reshape(2, 16, 1, 128)


def solution(mesh):
    split = Mesh(mesh.devices.reshape(mesh.shape["tm"], 4, 4, 2), ("tm", *PAR))
    placed = (P("tm", None, PAR), P("tm", PAR, None), P(None, "tm", PAR, None))
    return jax.shard_map(
        per_device,
        mesh=split,
        in_specs=placed,
        out_specs=P(None, None, ("tm", *PAR), None),
        check_vma=False,
    )
```

time: 130 us -> 53.1 us (0.41)
  blocking collectives: 54.9 us -> 0 us
  Pallas kernels: 0 us -> 49.1 us
  waiting for transfers between devices: 33.9 us -> 0 us
  starting transfers between devices: 18.6 us -> 0 us
  matrix products: 11.8 us -> 0 us
  local copies, waits for them, and re-layouts: 7.02 us -> 3.77 us
  other arithmetic: 2.27 us -> 0 us
    all_to_all x2 -> x0, blocking collectives: 54.9 us -> none  [the longest x1 32.8 us: sent_and_summed(): lax.all_to_all(parts, axis, split_axis=0, concat_axis=0, tiled=True)]
    pallas_call x0 -> x1, Pallas kernels: none -> 49.1 us  [per_device(): pl.pallas_call(kernel, out_shape=jax.ShapeDtypeStruct((32, 128), bf16), i...]
    all_to_all x1 -> x0, waiting for transfers between devices: 22.8 us -> none  [from_everyone(): return lax.all_to_all(copies, axis, split_axis=0, concat_axis=0, tiled=True)]
    dot_general x16 -> x0, matrix products: 11.8 us -> none  [the longest x8 3.6 us: product(): jnp.einsum('njy,nyv->njv', left_operand, right_operand, preferred_element...]
    ppermute x2 -> x0, waiting for transfers between devices: 11 us -> none  [from_behind(): return lax.ppermute(array, axis, pairs)]
    ppermute x2 -> x0, starting transfers between devices: 9.59 us -> none  [from_behind(): return lax.ppermute(array, axis, pairs)]
    all_to_all x1 -> x0, starting transfers between devices: 9 us -> none  [from_everyone(): return lax.all_to_all(copies, axis, split_axis=0, concat_axis=0, tiled=True)]
    broadcast_in_dim x1 -> x0, local copies, waits for them, and re-layouts: 2.29 us -> none  [from_everyone(): copies = jnp.broadcast_to(array, (lax.axis_size(axis), *array.shape))]
  transfers between devices with their start and end apart: 3 -> 0, of which waited for: 3 -> 0; matrix products, arithmetic and copies ran while one was open for 3% -> 0% of each run, Pallas kernels for 0% -> 0%
where the time goes in v1:
time: 53.1 us; the launch traced here: 52.9 us
  Pallas kernels  49.1 us (92%)
  local copies, waits for them, and re-layouts  3.77 us (7%)
    pallas_call x1, Pallas kernels, per_device(): pl.pallas_call(kernel, out_shape=jax.ShapeDtypeStruct((32, 128), bf16), i...  49.1 us
    unnamed x7, local copies, waits for them, and re-layouts  3.77 us

profile of v1, /device:TPU:1, one launch (start us, length us, event | category | flops | bytes accessed | tf_op | source)
XLA Modules:
  0.0 52.9 jit_solution(6842115592505521133)
XLA Ops:
  0.0 0.0 copy-start
  0.0 1.2 %copy-done = bf16[16,256,128]{2,1,0:T(8,128)(2,1)S(1)} copy-done((bf16[16,256,128]{2,1,0:T(8,128)(2,1)S(1)}, bf16[16,256,128]{2,1,0:T(8,128)(2,1)}, u32[]{:S(2)}) %copy-start) | copy-done | bytes 1048600
  1.2 0.0 copy-start.1
  1.2 1.0 %copy-done.1 = bf16[16,128,128]{2,1,0:T(8,128)(2,1)S(1)} copy-done((bf16[16,128,128]{2,1,0:T(8,128)(2,1)S(1)}, bf16[16,128,128]{2,1,0:T(8,128)(2,1)}, u32[]{:S(2)}) %copy-start.1) | copy-done | bytes 524312
  2.3 0.0 copy-start.2
  2.3 0.9 %copy-done.2 = bf16[2,2,128,128]{3,2,1,0:T(8,128)(2,1)S(1)} copy-done((bf16[2,2,128,128]{3,2,1,0:T(8,128)(2,1)S(1)}, bf16[2,2,128,128]{3,2,1,0:T(8,128)(2,1)}, u32[]{:S(2)}) %copy-start.2) | copy-done | bytes 131096
  3.2 49.1 %shard_map.37 = bf16[32,128]{1,0:T(8,128)(2,1)S(1)} custom-call(bf16[16,256,128]{2,1,0:T(8,128)(2,1)S(1)} %copy-done, bf16[16,128,128]{2,1,0:T(8,128)(2,1)S(1)} %copy-done.1, bf16[2,2,128,128]{3,2,1,0:T(8,128)(2,1)S(1)} %copy-done.2), custom_call_target="tpu_custom_call" | custom-call | tf_op jit(solution)/shard_map/pallas_call | solution.py:280
  52.3 0.6 %copy.6 = bf16[2,16,1,128]{3,1,2,0:T(8,128)(2,1)} copy(bf16[2,16,1,128]{3,1,2,0:T(8,128)(2,1)S(1)} %bitcast.3) | data formatting | bytes 16384
Async XLA Ops:
  0.0 1.2 %copy-start = (bf16[16,256,128]{2,1,0:T(8,128)(2,1)S(1)}, bf16[16,256,128]{2,1,0:T(8,128)(2,1)}, u32[]{:S(2)}) copy-start(bf16[16,256,128]{2,1,0:T(8,128)(2,1)} %k_hbm.1) | copy-start | bytes 3145732
  1.2 1.0 %copy-start.1 = (bf16[16,128,128]{2,1,0:T(8,128)(2,1)S(1)}, bf16[16,128,128]{2,1,0:T(8,128)(2,1)}, u32[]{:S(2)}) copy-start(bf16[16,128,128]{2,1,0:T(8,128)(2,1)} %h_hbm.1) | copy-start | bytes 1572868
  2.3 0.9 %copy-start.2 = (bf16[2,2,128,128]{3,2,1,0:T(8,128)(2,1)S(1)}, bf16[2,2,128,128]{3,2,1,0:T(8,128)(2,1)}, u32[]{:S(2)}) copy-start(bf16[2,2,128,128]{3,2,1,0:T(8,128)(2,1)} %a_hbm.1) | copy-start | bytes 393220

commit v2 on v1

v2 whole, which is shorter than its diff:
```python
import jax
import jax.numpy as jnp
from jax import lax
from jax.experimental import pallas as pl
from jax.experimental.pallas import tpu as pltpu
from jax.sharding import Mesh
from jax.sharding import PartitionSpec as P

PAR = ("px", "py", "pc")
MESH = pl.DeviceIdType.MESH
CHUNKS = [(4 * g, 4) for g in range(7)] + [(28, 2), (30, 2)]
WIDE = 4 * 128
PLAN = (
    ("A", 0), ("P", 0), ("S", 1), ("A", 1), ("Q", 1), ("B", 0), ("R", 0), ("B", 1), ("A", 2), ("B", 2), ("A", 3),
    ("T", 0), ("R", 1), ("C", 0), ("B", 3), ("A", 4), ("C", 1), ("B", 4), ("A", 5), ("C", 2), ("D", 0), ("B", 5),
    ("A", 6), ("C", 3), ("D", 1), ("A", 7), ("B", 6), ("C", 4), ("A", 8), ("B", 7), ("B", 8), ("D", 2), ("D", 3),
    ("Z", 0), ("C", 5), ("C", 6), ("C", 7), ("C", 8), ("D", 4), ("D", 5), ("D", 6), ("D", 7), ("D", 8), ("Z", 1),
    ("E", 0), ("F", 0), ("F", 1), ("E", 1),
)


def kernel(k_hbm, h_hbm, a_hbm, out_ref, kv, krev, w, w2, arr, relay, d2s, d2o, d2r, s1, o1, r1, s2, o2, r2, yb, zs, zo, zr,
           rounds, local_sem, w_recv, own_send, fwd_send, arr_send, relay_recv, relay_send, d2_send, d2_recv,
           s1_send, s1_recv, s2_send, s2_recv, z_send, z_recv):
    z, x, y, c = (lax.axis_index(name) for name in ("tm", "px", "py", "pc"))
    nz, nx, ny, nc = 8, 4, 4, 2
    chunks = len(CHUNKS)
    sizes = {"tm": nz, "px": nx, "py": ny, "pc": nc}
    here = {"tm": z, "px": x, "py": y, "pc": c}

    def ahead(name, by):
        return {name: lax.rem(here[name] + by, sizes[name])}

    copy_k = pltpu.make_async_copy(k_hbm, kv, local_sem.at[0])
    copy_k.start()
    copy_h = pltpu.make_async_copy(h_hbm, w.at[pl.ds(0, 16)], local_sem.at[1])
    copy_h.start()
    copy_a = pltpu.make_async_copy(a_hbm, arr, local_sem.at[2])
    copy_a.start()

    barrier = pltpu.get_barrier_semaphore()
    plane = [("px", 1), ("px", nx - 1), ("py", 1), ("py", ny - 1)]

    def greet(sem, peers):
        for name, by in peers:
            pl.semaphore_signal(sem, inc=1, device_id=ahead(name, by), device_id_type=MESH)

    @pl.when(z > 0)
    def _():
        greet(barrier, [("tm", nz - 1)])

    for by in (1, 2, 3):

        @pl.when(z + by < nz)
        def _():
            greet(barrier, [("tm", by)])

    @pl.when(z == 0)
    def _():
        greet(barrier, [("tm", nz - 1)])

    greet(barrier, plane + [("pc", 1)])
    for count in (1, 2, 3):

        @pl.when(z == count - 1)
        def _():
            pl.semaphore_wait(barrier, 5 + count)

    @pl.when(z >= 3)
    def _():
        pl.semaphore_wait(barrier, 5 + 4)

    def remote(src, dst, send_sem, recv_sem, target):
        return pltpu.make_async_remote_copy(
            src_ref=src, dst_ref=dst, send_sem=send_sem, recv_sem=recv_sem, device_id=target, device_id_type=MESH
        )

    def own_piece(i):
        return remote(
            w.at[pl.ds(2 * i, 2)], w.at[pl.ds(16 + 2 * i, 2)], own_send.at[0], w_recv.at[0, i], ahead("tm", 1)
        )

    def forward_piece(i):
        return remote(
            w.at[pl.ds(16 + 2 * i, 2)], w.at[pl.ds(32 + 2 * i, 2)], fwd_send.at[0], w_recv.at[1, i], ahead("tm", 1)
        )

    def wait_piece(blk, i):
        ref = w.at[pl.ds(16 + 16 * blk + 2 * i, 2)]
        remote(ref, ref, fwd_send.at[0], w_recv.at[blk, i], ahead("tm", 1)).wait_recv()

    def arrival_piece(s, owner):
        return remote(
            arr.at[s], w.at[pl.ds(16 + 16 * s + 2 * owner, 2)], arr_send.at[s], w_recv.at[s, owner], {"tm": 0}
        )

    def to_relay(s):
        return remote(arr.at[s], relay.at[s], arr_send.at[s], relay_recv.at[s], ahead("tm", nz - 3))

    def from_relay(s, owner):
        return remote(
            relay.at[s], w.at[pl.ds(16 + 16 * s + 2 * owner, 2)], relay_send.at[s], w_recv.at[s, owner], {"tm": 0}
        )

    def local_arrival(s):
        return pltpu.make_async_copy(a_hbm.at[s], w.at[pl.ds(16 + 16 * s, 2)], w_recv.at[s, 0])

    @pl.when(z == 0)
    def _():
        for s in range(2):
            local_arrival(s).start()

    def send_direct(s):
        for owner in (1, 2, 3, 7):

            @pl.when(z == owner)
            def _():
                arrival_piece(s, owner).start()

    def send_to_relay(s):
        @pl.when((z >= 4) & (z <= 6))
        def _():
            to_relay(s).start()

    greet(rounds.at[0], plane)
    copy_h.wait()

    @pl.when(z < nz - 1)
    def _():
        for i in range(8):
            own_piece(i).start()

    copy_a.wait()
    send_direct(0)
    send_to_relay(0)

    row = lax.broadcasted_iota(jnp.int32, (256, 256), 0)
    col = lax.broadcasted_iota(jnp.int32, (256, 256), 1)
    core_of = (c + (row >> 7)) & 1
    x_of = (x + (row >> 5)) & 3
    y_of = (y + (row >> 3)) & 3
    z_of = (z + row) & 7
    sensor = z_of * 32 + x_of * 8 + y_of * 2 + core_of
    order = jnp.where(sensor == col, 1.0, 0.0).astype(jnp.bfloat16)
    copy_k.wait()
    for lag in range(16):
        moved = jnp.dot(order, kv[lag], preferred_element_type=jnp.float32)
        krev[:, (15 - lag) * 128 : (16 - lag) * 128] = moved.astype(jnp.bfloat16)

    def place(t):
        block = w[t]
        w2[t * 128 : (t + 1) * 128, 0:128] = block
        if t > 0:
            w2[(t - 1) * 128 : t * 128, 128:256] = block

    for t in range(16):
        place(t)

    def order_of(g):
        return ("px", "py") if g % 2 == 0 else ("py", "px")

    def lanes_of(g):
        return CHUNKS[g][1] * 128

    def core_copy(g):
        lanes = pl.ds(0, lanes_of(g))
        return remote(d2s.at[g, :, lanes], d2r.at[g, :, lanes], d2_send.at[0], d2_recv.at[g], ahead("pc", 1))

    def first_copy(g, d):
        lanes = pl.ds(0, lanes_of(g))
        return remote(
            s1.at[g, d - 1, :, lanes],
            r1.at[g, d - 1, :, lanes],
            s1_send.at[0],
            s1_recv.at[g],
            ahead(order_of(g)[0], d),
        )

    def second_copy(g, d):
        lanes = pl.ds(0, lanes_of(g) // 2)
        return remote(
            s2.at[g, d - 1, :, lanes],
            r2.at[g, d - 1, :, lanes],
            s2_send.at[0],
            s2_recv.at[g],
            ahead(order_of(g)[1], d),
        )

    def z_copy(s, d):
        return remote(zs.at[s, d - 1], zr.at[s, d - 1], z_send.at[0], z_recv.at[s], ahead("tm", d))

    def landed(ref, sem):
        remote(ref, ref, z_send.at[0], sem, ahead("tm", 1)).wait_recv()

    def left(ref, sem):
        remote(ref, ref, sem, z_recv.at[0], ahead("tm", 1)).wait_send()

    def compute(g):
        first, size = CHUNKS[g]
        blk = first // 16

        def part(m, low, high, rows=slice(0, 256)):
            return jnp.dot(
                krev[rows, low * 128 : high * 128],
                w2[(m + 1 + low) * 128 : (m + 1 + high) * 128, :],
                preferred_element_type=jnp.float32,
            )

        mine, other = slice(0, 128), slice(128, 256)
        if size == 2:
            early_other, early_mine = part(first, 0, 14, other), part(first, 0, 14, mine)
        for i in range((first % 16) // 2, (first % 16 + size) // 2):
            wait_piece(blk, i)
            if blk == 0:

                @pl.when(z < nz - 1)
                def _():
                    forward_piece(i).start()

            for t in range(16 + 16 * blk + 2 * i, 18 + 16 * blk + 2 * i):
                place(t)
        if size == 2:
            d2s[g, :, :256] = (early_other + part(first, 14, 16, other)).astype(jnp.bfloat16)
            core_copy(g).start()
            d2o[g, :, :256] = early_mine + part(first, 14, 16, mine)
            return
        for pair in range(size // 2):
            m = first + 2 * pair
            found = part(m, 0, 16)
            d2s[g, :, pair * 256 : (pair + 1) * 256] = found[128:].astype(jnp.bfloat16)
            d2o[g, :, pair * 256 : (pair + 1) * 256] = found[:128]
        core_copy(g).start()

    def fold(block):
        half = block.shape[1] // 2
        return jnp.concatenate([block[:, :half], block[:, half:]], axis=0)

    def after_core(g):
        lanes = lanes_of(g)
        core_copy(g).wait_recv()
        total = d2o[g, :, :lanes] + d2r[g, :, :lanes].astype(jnp.float32)
        for d in range(4):
            if order_of(g)[0] == "px":
                block = total[32 * d : 32 * d + 32]
            else:
                block = jnp.concatenate([total[32 * e + 8 * d : 32 * e + 8 * d + 8] for e in range(4)], axis=0)
            if d == 0:
                o1[g, :, :lanes] = block
            else:
                s1[g, d - 1, :, :lanes] = block.astype(jnp.bfloat16)
        for d in (2, 1, 3):
            first_copy(g, d).start()

    def after_first(g):
        lanes = lanes_of(g)
        total = o1[g, :, :lanes]
        landed(r1.at[g, :, :, pl.ds(0, lanes)], s1_recv.at[g])
        for d in (1, 3, 2):
            total = total + r1[g, d - 1, :, :lanes].astype(jnp.float32)
        for d in range(4):
            block = fold(total[8 * d : 8 * d + 8])
            if d == 0:
                o2[g, :, : lanes // 2] = block
            else:
                s2[g, d - 1, :, : lanes // 2] = block.astype(jnp.bfloat16)
        for d in (2, 1, 3):
            second_copy(g, d).start()

    def after_second(g):
        first, size = CHUNKS[g]
        lanes = lanes_of(g) // 2
        total = o2[g, :, :lanes]
        landed(r2.at[g, :, :, pl.ds(0, lanes)], s2_recv.at[g])
        for d in (1, 3, 2):
            total = total + r2[g, d - 1, :, :lanes].astype(jnp.float32)
        for high in range(2):
            for low in range(size // 2):
                m = first + high * (size // 2) + low
                yb[m * 8 : m * 8 + 8, :] = total[high * 8 : high * 8 + 8, low * 128 : (low + 1) * 128]

    def meet_plane(_):
        pl.semaphore_wait(rounds.at[0], len(plane))

    def tell_all(_):
        @pl.when(z == 0)
        def _():
            greet(rounds.at[1], [("tm", by) for by in range(1, nz)])

    def send_z(s):
        if s == 0:

            @pl.when(z > 0)
            def _():
                pl.semaphore_wait(rounds.at[1], 1)

        for d in range(8):
            rows = yb[pl.ds(s * 128 + d, 16, stride=8), :]
            if d == 0:
                zo[s] = rows
            else:
                zs[s, d - 1] = rows.astype(jnp.bfloat16)
        for d in (4, 3, 5, 2, 6, 1, 7):
            z_copy(s, d).start()

    def finish(s):
        total = zo[s]
        landed(zr.at[s], z_recv.at[s])
        for d in range(1, 8):
            total = total + zr[s, d - 1].astype(jnp.float32)
        out_ref[s * 16 : (s + 1) * 16, :] = total.astype(jnp.bfloat16)

    def relay_on(s):
        for owner in (4, 5, 6):

            @pl.when(z == owner - 3)
            def _():
                to_relay(s).wait_recv()
                from_relay(s, owner).start()

    def end_sends(part):
        if part == 1:
            left(zs, z_send.at[0])
            return

        @pl.when(z < nz - 1)
        def _():
            left(w.at[pl.ds(0, 16)], own_send.at[0])
            left(w.at[pl.ds(16, 16)], fwd_send.at[0])

        for s in range(2):
            for owner in (1, 2, 3, 7):

                @pl.when(z == owner)
                def _():
                    arrival_piece(s, owner).wait_send()

            for owner in (4, 5, 6):

                @pl.when(z == owner)
                def _():
                    to_relay(s).wait_send()

                @pl.when(z == owner - 3)
                def _():
                    from_relay(s, owner).wait_send()

        left(d2s.at[pl.ds(0, chunks - 1)], d2_send.at[0])
        left(s1.at[pl.ds(0, chunks - 1)], s1_send.at[0])
        left(s2.at[pl.ds(0, chunks - 1)], s2_send.at[0])

    stages = {"A": compute, "B": after_core, "C": after_first, "D": after_second, "R": relay_on, "Z": send_z, "F": finish, "S": send_direct, "Q": send_to_relay}
    stages |= {"P": meet_plane, "T": tell_all, "E": end_sends}
    for stage, number in PLAN:
        stages[stage](number)


def per_device(lags, history, arrivals):
    chunks, lanes = len(CHUNKS), WIDE
    bf16, f32 = jnp.bfloat16, jnp.float32
    dma = pltpu.SemaphoreType.DMA
    found = pl.pallas_call(
        kernel,
        out_shape=jax.ShapeDtypeStruct((32, 128), bf16),
        in_specs=[pl.BlockSpec(memory_space=pltpu.HBM)] * 3,
        out_specs=pl.BlockSpec(memory_space=pltpu.VMEM),
        scratch_shapes=[
            pltpu.VMEM((16, 256, 128), bf16),
            pltpu.VMEM((256, 2048), bf16),
            pltpu.VMEM((48, 128, 128), bf16),
            pltpu.VMEM((48 * 128, 256), bf16),
            pltpu.VMEM((2, 2, 128, 128), bf16),
            pltpu.VMEM((2, 2, 128, 128), bf16),
            pltpu.VMEM((chunks, 128, lanes), bf16),
            pltpu.VMEM((chunks, 128, lanes), f32),
            pltpu.VMEM((chunks, 128, lanes), bf16),
            pltpu.VMEM((chunks, 3, 32, lanes), bf16),
            pltpu.VMEM((chunks, 32, lanes), f32),
            pltpu.VMEM((chunks, 3, 32, lanes), bf16),
            pltpu.VMEM((chunks, 3, 16, lanes // 2), bf16),
            pltpu.VMEM((chunks, 16, lanes // 2), f32),
            pltpu.VMEM((chunks, 3, 16, lanes // 2), bf16),
            pltpu.VMEM((256, 128), f32),
            pltpu.VMEM((2, 7, 16, 128), bf16),
            pltpu.VMEM((2, 16, 128), f32),
            pltpu.VMEM((2, 7, 16, 128), bf16),
            pltpu.SemaphoreType.REGULAR((2,)),
            dma((3,)),
            dma((2, 8)),
            dma((1,)),
            dma((1,)),
            dma((2,)),
            dma((2,)),
            dma((2,)),
            dma((1,)),
            dma((chunks,)),
            dma((1,)),
            dma((chunks,)),
            dma((1,)),
            dma((chunks,)),
            dma((1,)),
            dma((2,)),
        ],
        compiler_params=pltpu.CompilerParams(
            collective_id=0, has_side_effects=True, vmem_limit_bytes=55168 * 1024
        ),
    )(lags, history, arrivals)
    return found.reshape(2, 16, 1, 128)


def solution(mesh):
    split = Mesh(mesh.devices.reshape(mesh.shape["tm"], 4, 4, 2), ("tm", *PAR))
    placed = (P("tm", None, PAR), P("tm", PAR, None), P(None, "tm", PAR, None))
    return jax.shard_map(
        per_device,
        mesh=split,
        in_specs=placed,
        out_specs=P(None, None, ("tm", *PAR), None),
        check_vma=False,
    )
```

time: 53.1 us -> 46.7 us (0.88)
  Pallas kernels: 49.1 us -> 45.5 us
  local copies, waits for them, and re-layouts: 3.77 us -> 0.6 us
    pallas_call x1, Pallas kernels: 49.1 us -> 45.5 us  [per_device(): pl.pallas_call(kernel, out_shape=jax.ShapeDtypeStruct((32, 128), bf16), i...]
    unnamed x7 -> x1, local copies, waits for them, and re-layouts: 3.77 us -> 0.6 us
where the time goes in v2:
time: 46.7 us; the launch traced here: 46.1 us
  Pallas kernels  45.5 us (97%)
  local copies, waits for them, and re-layouts  0.6 us (1%)
    pallas_call x1, Pallas kernels, per_device(): pl.pallas_call(kernel, out_shape=jax.ShapeDtypeStruct((32, 128), bf16), i...  45.5 us

profile of v2, /device:TPU:1, one launch (start us, length us, event | category | flops | bytes accessed | tf_op | source)
XLA Modules:
  0.0 46.1 jit_solution(9230942788248364697)
XLA Ops:
  0.0 45.5 %shard_map.37 = bf16[32,128]{1,0:T(8,128)(2,1)S(1)} custom-call(bf16[16,256,128]{2,1,0:T(8,128)(2,1)} %k_hbm.1, bf16[16,128,128]{2,1,0:T(8,128)(2,1)} %h_hbm.1, bf16[2,2,128,128]{3,2,1,0:T(8,128)(2,1)} %a_hbm.1), custom_call_target="tpu_custom_call" | custom-call | tf_op jit(solution)/shard_map/pallas_call | solution.py:361
  45.5 0.6 %copy.6 = bf16[2,16,1,128]{3,1,2,0:T(8,128)(2,1)} copy(bf16[2,16,1,128]{3,1,2,0:T(8,128)(2,1)S(1)} %bitcast.3) | data formatting | bytes 16384

commit v3 on v2

--- a/solution.py
+++ b/solution.py
@@ -8,19 +8,39 @@
 
 PAR = ("px", "py", "pc")
 MESH = pl.DeviceIdType.MESH
-CHUNKS = [(4 * g, 4) for g in range(7)] + [(28, 2), (30, 2)]
+CHUNKS = [(4 * g, 4) for g in range(6)] + [(24, 2), (26, 2), (28, 2), (30, 2)]
+WHOLE = 8
+PIECES = (8, 8, 7, 7, 6, 6, 5, 5)
+LAGS = tuple(16 - 2 * n for n in PIECES)
+MOST = max(LAGS)
 WIDE = 4 * 128
 PLAN = (
-    ("A", 0), ("P", 0), ("S", 1), ("A", 1), ("Q", 1), ("B", 0), ("R", 0), ("B", 1), ("A", 2), ("B", 2), ("A", 3),
-    ("T", 0), ("R", 1), ("C", 0), ("B", 3), ("A", 4), ("C", 1), ("B", 4), ("A", 5), ("C", 2), ("D", 0), ("B", 5),
-    ("A", 6), ("C", 3), ("D", 1), ("A", 7), ("B", 6), ("C", 4), ("A", 8), ("B", 7), ("B", 8), ("D", 2), ("D", 3),
-    ("Z", 0), ("C", 5), ("C", 6), ("C", 7), ("C", 8), ("D", 4), ("D", 5), ("D", 6), ("D", 7), ("D", 8), ("Z", 1),
-    ("E", 0), ("F", 0), ("F", 1), ("E", 1),
+    ("A", 0), ("P", 0), ("S", 1), ("Q", 1), ("A", 1), ("B", 0), ("R", 0), ("B", 1), ("A", 2), ("B", 2), ("A", 3),
+    ("C", 0), ("B", 3), ("R", 1), ("A", 4), ("C", 1), ("V", 6), ("V", 7), ("V", 8), ("V", 9), ("B", 4), ("K", 0),
+    ("C", 2), ("D", 0), ("A", 5), ("U", 6), ("U", 7), ("U", 8), ("U", 9), ("C", 3), ("A", 6), ("B", 5), ("A", 7),
+    ("A", 8), ("B", 6), ("A", 9), ("B", 7), ("B", 8), ("B", 9), ("D", 1), ("D", 2), ("C", 4), ("D", 3), ("Z", 0),
+    ("C", 6), ("C", 5), ("C", 8), ("C", 7), ("C", 9), ("D", 4), ("D", 5), ("D", 6), ("D", 7), ("D", 8), ("D", 9),
+    ("Z", 1), ("E", 0), ("F", 0), ("F", 1), ("E", 1),
 )
-
-
-def kernel(k_hbm, h_hbm, a_hbm, out_ref, kv, krev, w, w2, arr, relay, d2s, d2o, d2r, s1, o1, r1, s2, o2, r2, yb, zs, zo, zr,
-           rounds, local_sem, w_recv, own_send, fwd_send, arr_send, relay_recv, relay_send, d2_send, d2_recv,
+LAST = (
+    ("A", 0), ("P", 0), ("S", 1), ("A", 1), ("B", 0), ("B", 1), ("A", 2), ("B", 2), ("A", 3), ("C", 0), ("B", 3),
+    ("A", 4), ("C", 1), ("V", 6), ("V", 7), ("V", 8), ("V", 9), ("B", 4), ("C", 2), ("D", 0), ("A", 5), ("C", 3),
+    ("N", 6), ("B", 5), ("N", 7), ("N", 8), ("B", 6), ("N", 9), ("B", 7), ("B", 8), ("B", 9), ("D", 1), ("D", 2),
+    ("C", 4), ("D", 3), ("Z", 0), ("C", 6), ("C", 5), ("C", 8), ("C", 7), ("C", 9), ("D", 4), ("D", 5), ("D", 6),
+    ("D", 7), ("D", 8), ("D", 9), ("Z", 1), ("E", 0), ("F", 0), ("F", 1), ("E", 1),
+)
+FIRST = (
+    ("A", 0), ("P", 0), ("A", 1), ("B", 0), ("B", 1), ("C", 0), ("C", 1), ("A", 2), ("A", 3), ("T", 0), ("B", 2),
+    ("A", 4), ("B", 3), ("V", 6), ("V", 7), ("V", 8), ("V", 9), ("B", 4), ("K", 0), ("A", 5), ("U", 6), ("U", 7),
+    ("U", 8), ("U", 9), ("B", 5), ("D", 0), ("D", 1), ("A", 6), ("A", 7), ("C", 2), ("A", 8), ("B", 6), ("A", 9),
+    ("B", 7), ("B", 8), ("B", 9), ("C", 3), ("C", 4), ("C", 6), ("C", 5), ("D", 2), ("D", 3), ("Z", 0), ("C", 8),
+    ("C", 7), ("C", 9), ("D", 4), ("D", 5), ("D", 6), ("D", 7), ("D", 8), ("D", 9), ("Z", 1), ("E", 0), ("F", 0),
+    ("F", 1), ("E", 1),
+)
+
+
+def kernel(k_hbm, h_hbm, a_hbm, out_ref, kv, kx, krev, kxrev, orders, acc, v2, w, w2, arr, relay, d2s, d2o, d2r, s1, o1, r1, s2, o2, r2, yb, zs, zo, zr,
+           rounds, local_sem, w_recv, own_send, fwd_send, arr_send, relay_recv, relay_send, kx_send, kx_recv, d2_send, d2_recv,
            s1_send, s1_recv, s2_send, s2_recv, z_send, z_recv):
     z, x, y, c = (lax.axis_index(name) for name in ("tm", "px", "py", "pc"))
     nz, nx, ny, nc = 8, 4, 4, 2
@@ -37,6 +57,10 @@
     copy_h.start()
     copy_a = pltpu.make_async_copy(a_hbm, arr, local_sem.at[2])
     copy_a.start()
+
+    kx[...] = jnp.zeros_like(kx)
+    w[48 - MOST :] = jnp.zeros((MOST, 128, 128), jnp.bfloat16)
+    v2[...] = jnp.zeros_like(v2)
 
     barrier = pltpu.get_barrier_semaphore()
     plane = [("px", 1), ("px", nx - 1), ("py", 1), ("py", ny - 1)]
@@ -141,10 +165,22 @@
     y_of = (y + (row >> 3)) & 3
     z_of = (z + row) & 7
     sensor = z_of * 32 + x_of * 8 + y_of * 2 + core_of
-    order = jnp.where(sensor == col, 1.0, 0.0).astype(jnp.bfloat16)
+    orders[...] = jnp.where(sensor == col, 1.0, 0.0).astype(jnp.bfloat16)
     copy_k.wait()
+
+    def lags_down(owner):
+        lags = pl.ds(0, LAGS[owner])
+        return remote(kv.at[lags], kx.at[lags], kx_send.at[0], kx_recv.at[0], {"tm": owner - 1})
+
+    for owner in range(1, nz):
+        if LAGS[owner]:
+
+            @pl.when(z == owner)
+            def _():
+                lags_down(owner).start()
+
     for lag in range(16):
-        moved = jnp.dot(order, kv[lag], preferred_element_type=jnp.float32)
+        moved = jnp.dot(orders[...], kv[lag], preferred_element_type=jnp.float32)
         krev[:, (15 - lag) * 128 : (16 - lag) * 128] = moved.astype(jnp.bfloat16)
 
     def place(t):
@@ -195,38 +231,78 @@
     def left(ref, sem):
         remote(ref, ref, sem, z_recv.at[0], ahead("tm", 1)).wait_send()
 
-    def compute(g):
+    def last_with(i):
+        return max(at for at in range(nz) if PIECES[at] > i)
+
+    def part(m, low, high, rows=slice(0, 256)):
+        return jnp.dot(
+            krev[rows, low * 128 : high * 128],
+            w2[(m + 1 + low) * 128 : (m + 1 + high) * 128, :],
+            preferred_element_type=jnp.float32,
+        )
+
+    def early(g):
+        m = CHUNKS[g][0]
+        acc[g] = part(m, 0, 34 - m)
+
+    def later(g):
+        m = CHUNKS[g][0]
+        acc[g] = acc[g] + part(m, 34 - m, 38 - m)
+
+    def given_lags(_):
+        for owner in range(1, nz):
+            if LAGS[owner]:
+
+                @pl.when(z == owner - 1)
+                def _():
+                    lags_down(owner).wait_recv()
+
+                    for u in range(LAGS[owner]):
+                        at = 2 * MOST - LAGS[owner] - 1 + u
+                        block = w[32 - LAGS[owner] + u]
+                        if at < 2 * MOST:
+                            v2[at * 128 : (at + 1) * 128, 0:128] = block
+                        v2[(at - 1) * 128 : at * 128, 128:256] = block
+
+        for lag in range(MOST):
+            moved = jnp.dot(orders[...], kx[lag], preferred_element_type=jnp.float32)
+            kxrev[:, (MOST - 1 - lag) * 128 : (MOST - lag) * 128] = moved.astype(jnp.bfloat16)
+        for g, (m, size) in enumerate(CHUNKS):
+            if m + 2 > 32 - MOST:
+                at = m - (32 - MOST)
+                acc[g] = acc[g] + jnp.dot(
+                    kxrev[...], v2[at * 128 : (at + MOST) * 128, :], preferred_element_type=jnp.float32
+                )
+
+    def compute(g, since=38):
         first, size = CHUNKS[g]
         blk = first // 16
-
-        def part(m, low, high, rows=slice(0, 256)):
-            return jnp.dot(
-                krev[rows, low * 128 : high * 128],
-                w2[(m + 1 + low) * 128 : (m + 1 + high) * 128, :],
-                preferred_element_type=jnp.float32,
-            )
-
-        mine, other = slice(0, 128), slice(128, 256)
-        if size == 2:
-            early_other, early_mine = part(first, 0, 14, other), part(first, 0, 14, mine)
         for i in range((first % 16) // 2, (first % 16 + size) // 2):
-            wait_piece(blk, i)
             if blk == 0:
-
-                @pl.when(z < nz - 1)
+                wait_piece(0, i)
+
+                @pl.when(z < last_with(i))
                 def _():
                     forward_piece(i).start()
+
+            elif last_with(i) == nz - 1:
+                wait_piece(1, i)
+            else:
+
+                @pl.when(z <= last_with(i))
+                def _():
+                    wait_piece(1, i)
 
             for t in range(16 + 16 * blk + 2 * i, 18 + 16 * blk + 2 * i):
                 place(t)
         if size == 2:
-            d2s[g, :, :256] = (early_other + part(first, 14, 16, other)).astype(jnp.bfloat16)
+            mine, other = slice(0, 128), slice(128, 256)
+            d2s[g, :, :256] = (acc[g, 128:] + part(first, since - first, 16, other)).astype(jnp.bfloat16)
             core_copy(g).start()
-            d2o[g, :, :256] = early_mine + part(first, 14, 16, mine)
+            d2o[g, :, :256] = acc[g, :128] + part(first, since - first, 16, mine)
             return
         for pair in range(size // 2):
-            m = first + 2 * pair
-            found = part(m, 0, 16)
+            found = part(first + 2 * pair, 0, 16)
             d2s[g, :, pair * 256 : (pair + 1) * 256] = found[128:].astype(jnp.bfloat16)
             d2o[g, :, pair * 256 : (pair + 1) * 256] = found[:128]
         core_copy(g).start()
@@ -322,10 +398,19 @@
             left(zs, z_send.at[0])
             return
 
-        @pl.when(z < nz - 1)
-        def _():
-            left(w.at[pl.ds(0, 16)], own_send.at[0])
-            left(w.at[pl.ds(16, 16)], fwd_send.at[0])
+        for at in range(nz - 1):
+
+            @pl.when(z == at)
+            def _():
+                left(w.at[pl.ds(0, 16)], own_send.at[0])
+                left(w.at[pl.ds(16, 2 * PIECES[at + 1])], fwd_send.at[0])
+
+        for owner in range(1, nz):
+            if LAGS[owner]:
+
+                @pl.when(z == owner)
+                def _():
+                    lags_down(owner).wait_send()
 
         for s in range(2):
             for owner in (1, 2, 3, 7):
@@ -344,14 +429,19 @@
                 def _():
                     from_relay(s, owner).wait_send()
 
-        left(d2s.at[pl.ds(0, chunks - 1)], d2_send.at[0])
-        left(s1.at[pl.ds(0, chunks - 1)], s1_send.at[0])
-        left(s2.at[pl.ds(0, chunks - 1)], s2_send.at[0])
-
-    stages = {"A": compute, "B": after_core, "C": after_first, "D": after_second, "R": relay_on, "Z": send_z, "F": finish, "S": send_direct, "Q": send_to_relay}
-    stages |= {"P": meet_plane, "T": tell_all, "E": end_sends}
-    for stage, number in PLAN:
-        stages[stage](number)
+        left(d2s.at[pl.ds(0, WHOLE)], d2_send.at[0])
+        left(s1.at[pl.ds(0, WHOLE)], s1_send.at[0])
+        left(s2.at[pl.ds(0, WHOLE)], s2_send.at[0])
+
+    inner = (z > 0) & (z < nz - 1)
+    stages = {"A": compute, "B": after_core, "C": after_first, "D": after_second, "R": relay_on, "Z": send_z, "F": finish, "S": send_direct}
+    stages |= {"P": meet_plane, "T": tell_all, "E": end_sends, "K": given_lags, "V": early, "U": later, "Q": send_to_relay, "N": lambda g: compute(g, 34)}
+    for here_now, plan in ((inner, PLAN), (z == 0, FIRST), (z == nz - 1, LAST)):
+
+        @pl.when(here_now)
+        def _():
+            for stage, number in plan:
+                stages[stage](number)
 
 
 def per_device(lags, history, arrivals):
@@ -365,7 +455,12 @@
         out_specs=pl.BlockSpec(memory_space=pltpu.VMEM),
         scratch_shapes=[
             pltpu.VMEM((16, 256, 128), bf16),
+            pltpu.VMEM((MOST, 256, 128), bf16),
             pltpu.VMEM((256, 2048), bf16),
+            pltpu.VMEM((256, MOST * 128), bf16),
+            pltpu.VMEM((256, 256), bf16),
+            pltpu.VMEM((chunks, 256, 256), f32),
+            pltpu.VMEM((2 * MOST * 128, 256), bf16),
             pltpu.VMEM((48, 128, 128), bf16),
             pltpu.VMEM((48 * 128, 256), bf16),
             pltpu.VMEM((2, 2, 128, 128), bf16),
@@ -392,6 +487,8 @@
             dma((2,)),
             dma((2,)),
             dma((1,)),
+            dma((1,)),
+            dma((1,)),
             dma((chunks,)),
             dma((1,)),
             dma((chunks,)),

time: 46.7 us -> 44.7 us (0.957)
  Pallas kernels: 45.5 us -> 43.8 us
    pallas_call x1, Pallas kernels: 45.5 us -> 43.8 us  [per_device(): pl.pallas_call(kernel, out_shape=jax.ShapeDtypeStruct((32, 128), bf16), i...]
where the time goes in v3:
time: 44.7 us; the launch traced here: 44.4 us
  Pallas kernels  43.8 us (98%)
  local copies, waits for them, and re-layouts  0.6 us (1%)
    pallas_call x1, Pallas kernels, per_device(): pl.pallas_call(kernel, out_shape=jax.ShapeDtypeStruct((32, 128), bf16), i...  43.8 us

profile of v3, /device:TPU:1, one launch (start us, length us, event | category | flops | bytes accessed | tf_op | source)
XLA Modules:
  0.0 44.4 jit_solution(9748427144709145616)
XLA Ops:
  0.0 43.8 %shard_map.37 = bf16[32,128]{1,0:T(8,128)(2,1)S(1)} custom-call(bf16[16,256,128]{2,1,0:T(8,128)(2,1)} %k_hbm.1, bf16[16,128,128]{2,1,0:T(8,128)(2,1)} %h_hbm.1, bf16[2,2,128,128]{3,2,1,0:T(8,128)(2,1)} %a_hbm.1), custom_call_target="tpu_custom_call" | custom-call | tf_op jit(solution)/shard_map/pallas_call | solution.py:451
  43.8 0.6 %copy.6 = bf16[2,16,1,128]{3,1,2,0:T(8,128)(2,1)} copy(bf16[2,16,1,128]{3,1,2,0:T(8,128)(2,1)S(1)} %bitcast.3) | data formatting | bytes 16384
